TPU v7x, 32 devices: a whole 2x2x4 slice. The times are simulated.
32 devices in a mesh: dp: 8 (over z, y), group: 4 (over x, core).
Axes of the slice: x: 2, y: 2, z: 4, core: 2. Of those that a mesh axis runs over, the one named last changes fastest.
Arguments:
- tokens: bfloat16 [16384, 1024], P(('dp', 'group')), may hold values from -16 to 16
- segment_ids: int32 [16384], P(('dp', 'group')), may hold values from 0 to 3, as said below
- positions: int32 [16384], P(('dp', 'group')), may hold values from 0 to 1999, as said below
- cotangent: bfloat16 [16384, 1024], P(('dp', 'group')), may hold values from -6 to 6
- qkv_weight: float32 [1024, 4096], P('group'), may hold values from -1 to 1
- out_weight: float32 [2048, 1024], P('group'), may hold values from -1 to 1
- gate_up_weight: float32 [1024, 6144], P('group'), may hold values from -0.1875 to 0.1875
- down_weight: float32 [3072, 1024], P('group'), may hold values from -0.109375 to 0.109375
- norm_gains: float32 [2, 1024], P(None, 'group'), may hold values from 0.5 to 1.5
- head_gains: float32 [2, 128], P(None, 'group'), may hold values from 0.6 to 1.4
- qkv_moments: float32 [2, 1024, 4096], P(None, 'group'), as said below
- out_moments: float32 [2, 2048, 1024], P(None, 'group'), as said below
- gate_up_moments: float32 [2, 1024, 6144], P(None, 'group'), as said below
- down_moments: float32 [2, 3072, 1024], P(None, 'group'), as said below
- norm_moments: float32 [2, 2, 1024], P(None, None, 'group'), as said below
- head_moments: float32 [2, 2, 128], P(None, None, 'group'), as said below
Outputs:
- output: bfloat16 [16384, 1024], P(('dp', 'group'))
- tokens_grad: bfloat16 [16384, 1024], P(('dp', 'group'))
- qkv_grad: float32 [1024, 4096], P('group', 'dp')
- out_grad: float32 [2048, 1024], P('group', 'dp')
- gate_up_grad: float32 [1024, 6144], P('group', 'dp')
- down_grad: float32 [3072, 1024], P('group', 'dp')
- norm_grad: float32 [2, 1024], P(None, 'group')
- head_grad: float32 [2, 128], P(None, 'group')
- new_qkv_weight: float32 [1024, 4096], P('group')
- new_out_weight: float32 [2048, 1024], P('group')
- new_gate_up_weight: float32 [1024, 6144], P('group')
- new_down_weight: float32 [3072, 1024], P('group')
- new_norm_gains: float32 [2, 1024], P(None, 'group')
- new_head_gains: float32 [2, 128], P(None, 'group')
- new_qkv_moments: float32 [2, 1024, 4096], P(None, 'group')
- new_out_moments: float32 [2, 2048, 1024], P(None, 'group')
- new_gate_up_moments: float32 [2, 1024, 6144], P(None, 'group')
- new_down_moments: float32 [2, 3072, 1024], P(None, 'group')
- new_norm_moments: float32 [2, 2, 1024], P(None, None, 'group')
- new_head_moments: float32 [2, 2, 128], P(None, None, 'group')
Inputs may be any that keep to these rules, and one draw needn't show every extreme that they name: `segment_ids`: along each sequence of 512 consecutive tokens the ids never fall; equal ids within a sequence mark one document. A token's position counts from its document's first token, which may lie in an earlier sequence; within a document positions rise by one. `qkv_moments`: the second moments are positive. `out_moments`: the second moments are positive. `gate_up_moments`: the second moments are positive. `down_moments`: the second moments are positive. `norm_moments`: the second moments are positive. `head_moments`: the second moments are positive.
All inputs are finite; a program needn't handle non-finite values.
Results may differ from a plain program's by a relative error of at most 0.013.
The roundings to bfloat16 on the way count: a program that leaves them out, or rounds other values in their place, can miss the bound.
Values may be sent and summed in bfloat16 or wider, within the bound.
A program may use at most 320 MiB of HBM per device.

v0:
```python
import math
import jax
import jax.numpy as jnp
from jax import lax
from jax.sharding import PartitionSpec as P

HQ = 16
HK = 8
HD = 128
FF = 3072
SEQ_LEN = 512
PARAMS = 15730944
EPS_NORM = 1e-06
ROPE_BASE = 1000000.0
MASKED = -1e30
LEARN_RATE = 0.03
GAIN_RATE = 0.3
WEIGHT_DECAY = 0.1
BETA_ONE = 0.9
BETA_TWO = 0.95
ADAM_EPS = 1e-08
STEP_COUNT = 3.0


def rotary_tables(places, width):
    half_width = width // 2
    frequency = ROPE_BASE ** (-(jnp.arange(half_width, dtype=jnp.float32) * 2.0) / width)
    angles = places.astype(jnp.float32)[:, None] * frequency[None, :]
    return (jnp.cos(angles), jnp.sin(angles))


def rotate(values, cosine, sine_table):
    half_width = values.shape[-1] // 2
    front_half = values[..., :half_width]
    back_half = values[..., half_width:]
    cosine = cosine[:, None, :]
    sine_table = sine_table[:, None, :]
    return jnp.concatenate(
        [
            front_half * cosine - back_half * sine_table,
            back_half * cosine + front_half * sine_table,
        ],
        axis=-1,
    )


def contract_rows(left_side, right_side):
    return lax.dot_general(
        left_side, right_side, (((0,), (0,)), ((), ())), preferred_element_type=jnp.float32
    )


def contract_cols(left_side, right_side):
    return lax.dot_general(
        left_side, right_side, (((1,), (1,)), ((), ())), preferred_element_type=jnp.float32
    )


def norm_back(grad_out, normed, inv_root, gain):
    scaled = grad_out * gain
    return inv_root * (scaled - normed * jnp.mean(normed * scaled, axis=-1, keepdims=True))


def joined_order(gradient, along, owners, copies):
    layout = gradient.shape
    pieces_shape = (
        layout[:along] + (owners, copies, layout[along] // (owners * copies)) + layout[along + 1 :]
    )
    return jnp.swapaxes(gradient.reshape(pieces_shape), along, along + 1).reshape(layout)


def own_columns(gradient, index, count):
    width = gradient.shape[1] // count
    return lax.dynamic_slice_in_dim(gradient, index * width, width, 1)


def adam_update(master, moment, gradient, factor, step_rate, decay_rate):
    clipped = gradient * factor
    first_moment = BETA_ONE * moment[0] + (1.0 - BETA_ONE) * clipped
    second = BETA_TWO * moment[1] + (1.0 - BETA_TWO) * clipped * clipped
    first_hat = first_moment / (1.0 - BETA_ONE**STEP_COUNT)
    second_hat = second / (1.0 - BETA_TWO**STEP_COUNT)
    renewed = master - step_rate * (
        first_hat / (jnp.sqrt(second_hat) + ADAM_EPS) + decay_rate * master
    )
    return (renewed, jnp.stack([first_moment, second]))


def on_device(
    tokens,
    segment_ids,
    positions,
    cotangent,
    qkv_weight,
    out_weight,
    gate_up_weight,
    down_weight,
    norm_gains,
    head_gains,
    qkv_moments,
    out_moments,
    gate_up_moments,
    down_moments,
    norm_moments,
    head_moments,
):
    full_qkv, full_out, full_gate_up, full_down, full_norm, full_head = (
        lax.all_gather(qkv_weight.astype(jnp.bfloat16), "group", axis=0, tiled=True),
        lax.all_gather(out_weight.astype(jnp.bfloat16), "group", axis=0, tiled=True),
        lax.all_gather(gate_up_weight.astype(jnp.bfloat16), "group", axis=0, tiled=True),
        lax.all_gather(down_weight.astype(jnp.bfloat16), "group", axis=0, tiled=True),
        lax.all_gather(norm_gains.astype(jnp.bfloat16), "group", axis=1, tiled=True),
        lax.all_gather(head_gains.astype(jnp.bfloat16), "group", axis=1, tiled=True),
    )
    token_rows = tokens.shape[0]
    seq_count = token_rows // SEQ_LEN
    groups = HQ // HK
    inv_head = 1.0 / math.sqrt(HD)
    gain_one = full_norm[0].astype(jnp.float32)
    gain_two = full_norm[1].astype(jnp.float32)
    gain_query = full_head[0].astype(jnp.float32)
    gain_key = full_head[1].astype(jnp.float32)
    inputs = tokens.astype(jnp.float32)
    root_one = lax.rsqrt(jnp.mean(inputs * inputs, axis=-1, keepdims=True) + EPS_NORM)
    normed_one = inputs * root_one
    hidden_one = (normed_one * gain_one).astype(jnp.bfloat16)
    projected = jnp.dot(hidden_one, full_qkv, preferred_element_type=jnp.float32)
    query_raw = projected[:, : HQ * HD].reshape(token_rows, HQ, HD)
    key_raw = projected[:, HQ * HD : (HQ + HK) * HD].reshape(token_rows, HK, HD)
    value_low = projected[:, (HQ + HK) * HD :].reshape(token_rows, HK, HD).astype(jnp.bfloat16)
    cosine, sine_table = rotary_tables(positions, HD)
    query_root = lax.rsqrt(jnp.mean(query_raw * query_raw, axis=-1, keepdims=True) + EPS_NORM)
    query_normed = query_raw * query_root
    query_low = rotate(query_normed * gain_query, cosine, sine_table).astype(jnp.bfloat16)
    key_root = lax.rsqrt(jnp.mean(key_raw * key_raw, axis=-1, keepdims=True) + EPS_NORM)
    key_normed = key_raw * key_root
    key_low = rotate(key_normed * gain_key, cosine, sine_table).astype(jnp.bfloat16)
    query_blocks = query_low.reshape(seq_count, SEQ_LEN, HK, groups, HD)
    key_blocks = key_low.reshape(seq_count, SEQ_LEN, HK, HD)
    value_blocks = value_low.reshape(seq_count, SEQ_LEN, HK, HD)
    seg_blocks = segment_ids.reshape(seq_count, SEQ_LEN)
    places_idx = jnp.arange(SEQ_LEN)
    allowed = (seg_blocks[:, :, None] == seg_blocks[:, None, :]) & (
        places_idx[:, None] >= places_idx[None, :]
    )[None]
    allowed = allowed[:, None, None, :, :]

    def scores_of():
        raw_scores = (
            jnp.einsum(
                "sqkgd,spkd->skgqp", query_blocks, key_blocks, preferred_element_type=jnp.float32
            )
            * inv_head
        )
        return jnp.where(allowed, raw_scores, MASKED)

    scores = scores_of()
    row_peak = jnp.max(scores, axis=-1, keepdims=True)
    exp_total = jnp.sum(jnp.exp(scores - row_peak), axis=-1, keepdims=True)
    log_total = row_peak + jnp.log(exp_total)
    probs_low = jnp.exp(scores - log_total).astype(jnp.bfloat16)
    mixed_heads = jnp.einsum(
        "skgqp,spkd->sqkgd", probs_low, value_blocks, preferred_element_type=jnp.float32
    )
    mixed_low = mixed_heads.reshape(token_rows, HQ * HD).astype(jnp.bfloat16)
    attended = jnp.dot(mixed_low, full_out, preferred_element_type=jnp.float32)
    residual = inputs + attended
    root_two = lax.rsqrt(jnp.mean(residual * residual, axis=-1, keepdims=True) + EPS_NORM)
    normed_two = residual * root_two
    hidden_two = (normed_two * gain_two).astype(jnp.bfloat16)
    gate_up = jnp.dot(hidden_two, full_gate_up, preferred_element_type=jnp.float32)
    gate_part = gate_up[:, :FF]
    upward = gate_up[:, FF:]
    sigmoid_gate = jax.nn.sigmoid(gate_part)
    activated = (gate_part * sigmoid_gate * upward).astype(jnp.bfloat16)
    branch = jnp.dot(activated, full_down, preferred_element_type=jnp.float32)
    output = (residual + branch).astype(jnp.bfloat16)
    upstream = cotangent.astype(jnp.float32)
    down_local = contract_rows(activated, cotangent)
    grad_act = contract_cols(cotangent, full_down)
    grad_gate = grad_act * upward * sigmoid_gate * (1.0 + gate_part * (1.0 - sigmoid_gate))
    grad_up = grad_act * gate_part * sigmoid_gate
    grad_gate_up = jnp.concatenate([grad_gate, grad_up], axis=-1).astype(jnp.bfloat16)
    gate_up_local = contract_rows(hidden_two, grad_gate_up)
    grad_hidden_two = contract_cols(grad_gate_up, full_gate_up)
    grad_gain_two = jnp.sum(grad_hidden_two * normed_two, axis=0)
    grad_residual = upstream + norm_back(grad_hidden_two, normed_two, root_two, gain_two)
    residual_low = grad_residual.astype(jnp.bfloat16)
    out_local = contract_rows(mixed_low, residual_low)
    grad_mixed = (
        contract_cols(residual_low, full_out)
        .astype(jnp.bfloat16)
        .reshape(seq_count, SEQ_LEN, HK, groups, HD)
    )
    attn_probs = jnp.exp(scores_of() - log_total)
    grad_probs = jnp.einsum(
        "sqkgd,spkd->skgqp", grad_mixed, value_blocks, preferred_element_type=jnp.float32
    )
    grad_value = jnp.einsum(
        "skgqp,sqkgd->spkd",
        attn_probs.astype(jnp.bfloat16),
        grad_mixed,
        preferred_element_type=jnp.float32,
    )
    grad_scores = (
        attn_probs * (grad_probs - jnp.sum(attn_probs * grad_probs, axis=-1, keepdims=True))
    ).astype(jnp.bfloat16)
    grad_query = (
        jnp.einsum("skgqp,spkd->sqkgd", grad_scores, key_blocks, preferred_element_type=jnp.float32)
        * inv_head
    )
    grad_key = (
        jnp.einsum(
            "skgqp,sqkgd->spkd", grad_scores, query_blocks, preferred_element_type=jnp.float32
        )
        * inv_head
    )
    grad_query = rotate(grad_query.reshape(token_rows, HQ, HD), cosine, -sine_table)
    grad_key = rotate(grad_key.reshape(token_rows, HK, HD), cosine, -sine_table)
    grad_gain_query = jnp.sum(grad_query * query_normed, axis=(0, 1))
    grad_gain_key = jnp.sum(grad_key * key_normed, axis=(0, 1))
    grad_query_raw = norm_back(grad_query, query_normed, query_root, gain_query)
    grad_key_raw = norm_back(grad_key, key_normed, key_root, gain_key)
    grad_projected = jnp.concatenate(
        [
            grad_query_raw.reshape(token_rows, HQ * HD),
            grad_key_raw.reshape(token_rows, HK * HD),
            grad_value.reshape(token_rows, HK * HD),
        ],
        axis=-1,
    ).astype(jnp.bfloat16)
    qkv_local = contract_rows(hidden_one, grad_projected)
    grad_hidden_one = contract_cols(grad_projected, full_qkv)
    grad_gain_one = jnp.sum(grad_hidden_one * normed_one, axis=0)
    grad_inputs = grad_residual + norm_back(grad_hidden_one, normed_one, root_one, gain_one)
    tokens_grad = grad_inputs.astype(jnp.bfloat16)
    norm_local = jnp.stack([grad_gain_one, grad_gain_two])
    head_local = jnp.stack([grad_gain_query, grad_gain_key])
    owners = lax.axis_size("group")
    copies = lax.axis_size("dp")
    pieces = (
        lax.psum_scatter(
            joined_order(qkv_local, 0, owners, copies),
            ("dp", "group"),
            scatter_dimension=0,
            tiled=True,
        ),
        lax.psum_scatter(
            joined_order(out_local, 0, owners, copies),
            ("dp", "group"),
            scatter_dimension=0,
            tiled=True,
        ),
        lax.psum_scatter(
            joined_order(gate_up_local, 0, owners, copies),
            ("dp", "group"),
            scatter_dimension=0,
            tiled=True,
        ),
        lax.psum_scatter(
            joined_order(down_local, 0, owners, copies),
            ("dp", "group"),
            scatter_dimension=0,
            tiled=True,
        ),
        lax.psum_scatter(
            joined_order(norm_local, 1, owners, copies),
            ("dp", "group"),
            scatter_dimension=1,
            tiled=True,
        ),
        lax.psum_scatter(
            joined_order(head_local, 1, owners, copies),
            ("dp", "group"),
            scatter_dimension=1,
            tiled=True,
        ),
    )
    summed = (
        lax.all_gather(pieces[0], "dp", axis=0, tiled=True),
        lax.all_gather(pieces[1], "dp", axis=0, tiled=True),
        lax.all_gather(pieces[2], "dp", axis=0, tiled=True),
        lax.all_gather(pieces[3], "dp", axis=0, tiled=True),
        lax.all_gather(pieces[4], "dp", axis=1, tiled=True),
        lax.all_gather(pieces[5], "dp", axis=1, tiled=True),
    )
    squares = sum((jnp.sum(gradient * gradient) for gradient in summed))
    grad_total = lax.psum(squares, "group")
    clip_limit = math.sqrt(PARAMS)
    factor = clip_limit / jnp.maximum(jnp.sqrt(grad_total), clip_limit)
    masters = (qkv_weight, out_weight, gate_up_weight, down_weight, norm_gains, head_gains)
    moments = (qkv_moments, out_moments, gate_up_moments, down_moments, norm_moments, head_moments)
    rates = (LEARN_RATE, LEARN_RATE, LEARN_RATE, LEARN_RATE, GAIN_RATE, GAIN_RATE)
    decays = (WEIGHT_DECAY, WEIGHT_DECAY, WEIGHT_DECAY, WEIGHT_DECAY, 0.0, 0.0)
    renewed_all = []
    moments_all = []
    for master, moment, gradient, step_rate, decay_rate in zip(
        masters, moments, summed, rates, decays
    ):
        renewed, stacked = adam_update(master, moment, gradient, factor, step_rate, decay_rate)
        renewed_all.append(renewed)
        moments_all.append(stacked)
    column_index = lax.axis_index("dp")
    column_count = lax.axis_size("dp")
    return (
        output,
        tokens_grad,
        own_columns(summed[0], column_index, column_count),
        own_columns(summed[1], column_index, column_count),
        own_columns(summed[2], column_index, column_count),
        own_columns(summed[3], column_index, column_count),
        summed[4],
        summed[5],
        renewed_all[0],
        renewed_all[1],
        renewed_all[2],
        renewed_all[3],
        renewed_all[4],
        renewed_all[5],
        moments_all[0],
        moments_all[1],
        moments_all[2],
        moments_all[3],
        moments_all[4],
        moments_all[5],
    )


def solution(mesh):
    placed = (
        P(("dp", "group"), None),
        P(("dp", "group")),
        P(("dp", "group")),
        P(("dp", "group"), None),
        P("group", None),
        P("group", None),
        P("group", None),
        P("group", None),
        P(None, "group"),
        P(None, "group"),
        P(None, "group", None),
        P(None, "group", None),
        P(None, "group", None),
        P(None, "group", None),
        P(None, None, "group"),
        P(None, None, "group"),
    )
    return jax.shard_map(
        on_device,
        mesh=mesh,
        in_specs=placed,
        out_specs=(
            P(("dp", "group"), None),
            P(("dp", "group"), None),
            P("group", "dp"),
            P("group", "dp"),
            P("group", "dp"),
            P("group", "dp"),
            P(None, "group"),
            P(None, "group"),
            P("group", None),
            P("group", None),
            P("group", None),
            P("group", None),
            P(None, "group"),
            P(None, "group"),
            P(None, "group", None),
            P(None, "group", None),
            P(None, "group", None),
            P(None, "group", None),
            P(None, None, "group"),
            P(None, None, "group"),
        ),
        check_vma=False,
    )
```

profile of v0, /device:TPU:0, one launch (start us, length us, event | category | flops | bytes accessed | tf_op | source)
XLA Modules:
  0.0 1525.3 jit_solution(2794801300747954)
XLA Ops:
  7.2 3.9 convert_element_type.111
  12.5 5.0 convert_element_type.126
  19.1 6.0 all_gather.36
  26.8 5.5 all-gather
  35.1 37.2 %all-gather.12.cloned.1.call-done = bf16[1024,4096]{1,0:T(8,128)(2,1)} async-done(((bf16[256,4096]{1,0:T(8,128)(2,1)}), bf16[1024,4096]{1,0:T(8,128)(2,1)}) %all-gather.12.cloned.1.call-update) | async-done | bytes 8388624 | tf_op jit(solution)/shard_map/all_gather | solution.py:108
  72.4 7.4 fusion.63
  80.5 3.2 copy-done.3
  93.9 2.7 fusion.46
  98.5 8.5 fusion.81
  107.0 8.2 exponential_reduce_fusion
  115.3 12.1 fusion.37
  127.4 6.5 multiply_reduce_fusion.9
  133.9 59.3 %all-gather.16.cloned.1.call-done = bf16[1024,6144]{1,0:T(8,128)(2,1)} async-done(((bf16[256,6144]{1,0:T(8,128)(2,1)}), bf16[1024,6144]{1,0:T(8,128)(2,1)}) %all-gather.16.cloned.1.call-update) | async-done | bytes 12582928 | tf_op jit(solution)/shard_map/all_gather | solution.py:110
  193.2 14.6 fusion.79
  207.9 33.8 %all-gather.18.cloned.1.call-done = bf16[3072,1024]{1,0:T(8,128)(2,1)} async-done(((bf16[768,1024]{1,0:T(8,128)(2,1)}), bf16[3072,1024]{1,0:T(8,128)(2,1)}) %all-gather.18.cloned.1.call-update) | async-done | bytes 6291472 | tf_op jit(solution)/shard_map/all_gather | solution.py:111
  241.6 13.2 multiply_convert_fusion.1
  254.9 14.3 multiply_reduce_fusion.6
  269.2 3.2 multiply_add_fusion.2
  274.8 4.1 copy.231
  279.2 10.4 fusion.82
  289.6 11.9 copy.233
  302.5 6.0 convolution_convert_fusion
  308.5 3.1 copy.266
  311.5 11.0 fusion
  322.6 12.8 fusion.5
  341.3 4.9 copy.263
  346.1 4.9 copy.264
  351.0 7.1 fusion.36
  359.7 3.0 fusion.54
  363.6 8.9 bitcast_convert_fusion
  373.1 4.9 multiply_subtract_fusion.2
  378.4 3.6 multiply_reduce_fusion.2
  387.4 7.8 fusion.11
  395.3 4.8 fusion.41
  400.0 6.3 copy.230
  408.0 15.1 fusion.12
  423.0 17.7 %copy.232 = f32[8,4,32,6144]{3,2,1,0:T(8,128)} copy(f32[8,4,32,6144]{3,2,0,1:T(8,128)} %bitcast.333) | data formatting | bytes 50331648 | tf_op jit(solution)/shard_map/transpose | solution.py:69
  442.4 10.6 fusion.29
  455.0 130.7 %reduce-scatter.15.cloned.1.call-done = f32[96,1024]{1,0:T(8,128)} async-done(((f32[3072,1024]{1,0:T(8,128)}), f32[96,1024]{1,0:T(8,128)}) %reduce-scatter.15.cloned.1.call-update) | async-done | bytes 393232 | tf_op jit(solution)/shard_map/reduce_scatter | solution.py:260
  585.7 184.1 %reduce-scatter.9.cloned.1.call-done = f32[32,4096]{1,0:T(8,128)} async-done(((f32[1024,4096]{1,0:T(8,128)}), f32[32,4096]{1,0:T(8,128)}) %reduce-scatter.9.cloned.1.call-update) | async-done | bytes 524304 | tf_op jit(solution)/shard_map/reduce_scatter | solution.py:242
  769.9 251.2 %reduce-scatter.13.cloned.1.call-done = f32[32,6144]{1,0:T(8,128)} async-done(((f32[1024,6144]{1,0:T(8,128)}), f32[32,6144]{1,0:T(8,128)}) %reduce-scatter.13.cloned.1.call-update) | async-done | bytes 786448 | tf_op jit(solution)/shard_map/reduce_scatter | solution.py:254
  1021.5 40.2 %all-reduce = f32[2,128]{1,0:T(2,128)S(1)} all-reduce(f32[2,128]{1,0:T(2,128)S(1)} %reshape.437), channel_id=7, replica_groups=mesh['dp'=8,'group'=4] {'dp','group'}, use_global_device_ids=true, to_apply=%region_22.23.clone | all-reduce | flops 256 | bytes 2048
  1061.8 20.0 %all-gather.2 = f32[8,4,2]{1,2,0:T(2,128)S(1)} all-gather(f32[1,4,2]{1,2,0:T(2,128)S(1)} %dynamic-slice_bitcast_fusion), channel_id=1, replica_groups=mesh['dp'=8,'group'=4] {'dp'}, dimensions={0}, use_global_device_ids=true | all-gather | bytes 288 | tf_op jit(solution)/shard_map/all_gather | solution.py:285
  1082.5 3.4 fusion.28
  1085.9 7.2 add_convert_fusion.1
  1093.1 66.1 %reduce-scatter.17.cloned.1.call-done = f32[32,2]{1,0:T(8,128)} async-done(((f32[1024,2]{1,0:T(8,128)}), f32[32,2]{1,0:T(8,128)}) %reduce-scatter.17.cloned.1.call-update) | async-done | bytes 272
  1160.0 16.3 %all-gather.1 = f32[8,32,2]{1,2,0:T(2,128)S(1)} all-gather(f32[1,32,2]{1,2,0:T(2,128)S(1)} %bitcast.382), channel_id=1, replica_groups=mesh['dp'=8,'group'=4] {'dp'}, dimensions={0}, use_global_device_ids=true | all-gather | bytes 2304 | tf_op jit(solution)/shard_map/all_gather | solution.py:284
  1177.0 29.3 %all-gather.22.cloned.1.call-done = f32[512,1024]{1,0:T(8,128)} async-done(((f32[64,1024]{1,0:T(8,128)}), f32[512,1024]{1,0:T(8,128)}) %all-gather.22.cloned.1.call-update) | async-done | bytes 2097168 | tf_op jit(solution)/shard_map/all_gather | solution.py:281
  1208.0 2.7 multiply_reduce_fusion.5
  1210.7 56.4 %all-gather.26.cloned.1.call-done = f32[768,1024]{1,0:T(8,128)} async-done(((f32[96,1024]{1,0:T(8,128)}), f32[768,1024]{1,0:T(8,128)}) %all-gather.26.cloned.1.call-update) | async-done | bytes 3145744 | tf_op jit(solution)/shard_map/all_gather | solution.py:283
  1268.9 3.3 multiply_reduce_fusion.4
  1272.2 68.4 %all-gather.20.cloned.1.call-done = f32[256,4096]{1,0:T(8,128)} async-done(((f32[32,4096]{1,0:T(8,128)}), f32[256,4096]{1,0:T(8,128)}) %all-gather.20.cloned.1.call-update) | async-done | bytes 4194320 | tf_op jit(solution)/shard_map/all_gather | solution.py:280
  1340.6 3.9 multiply_reduce_fusion.1
  1346.1 93.9 %all-gather.24.cloned.1.call-done = f32[256,6144]{1,0:T(8,128)} async-done(((f32[32,6144]{1,0:T(8,128)}), f32[256,6144]{1,0:T(8,128)}) %all-gather.24.cloned.1.call-update) | async-done | bytes 6291472 | tf_op jit(solution)/shard_map/all_gather | solution.py:282
  1440.0 5.0 multiply_reduce_fusion
  1449.5 6.4 psum.7
  1459.0 6.1 fusion.55
  1465.1 3.8 pad_maximum_fusion.3
  1470.3 13.3 fusion.45
  1483.6 10.9 pad_maximum_fusion
  1494.4 6.6 fusion.60
  1501.1 2.7 pad_maximum_fusion.6
  1506.1 6.9 fusion.53
  1513.0 4.4 pad_maximum_fusion.1
  (226 shorter events, 58.0 us)
Async XLA Ops:
  7.2 4.1 copy-start.18
  7.2 65.2 %all-gather.12.cloned.1.call-start = ((), (), s32[]{:S(2)}) async-start(), calls=%async_computation.5 | async-start | bytes 10485760 | tf_op jit(solution)/shard_map/all_gather | solution.py:108
  11.2 116.2 %all-gather.14.cloned.1.call-start = ((), (), s32[]{:S(2)}) async-start(), calls=%async_computation.6 | async-start | bytes 5242880 | tf_op jit(solution)/shard_map/all_gather | solution.py:109
  12.4 5.2 copy-start.11
  12.4 180.8 %all-gather.16.cloned.1.call-start = ((), (), s32[]{:S(2)}) async-start(), calls=%async_computation.7 | async-start | bytes 15728640 | tf_op jit(solution)/shard_map/all_gather | solution.py:110
  17.5 9.2 copy-start.53
  17.6 14.9 copy-start.51
  17.6 14.9 copy-start.45
  17.6 224.1 %all-gather.18.cloned.1.call-start = ((), (), s32[]{:S(2)}) async-start(), calls=%async_computation.8 | async-start | bytes 7864320 | tf_op jit(solution)/shard_map/all_gather | solution.py:111
  19.1 435.3 %reduce-scatter.11.cloned.1.call-start = ((), (), s32[]{:S(2)}) async-start(), calls=%async_computation.11 | async-start | bytes 8650752 | tf_op jit(solution)/shard_map/reduce_scatter | solution.py:248
  25.2 54.6 %copy-start.39 = (f32[1,1024]{1,0:T(1,128)}, f32[1,1024]{1,0:T(1,128)S(1)}, u32[]{:S(2)}) copy-start(f32[1,1024]{1,0:T(1,128)S(1)} %get-tuple-element.63) | copy-start | bytes 12292
  26.8 53.0 %copy-start.42 = (f32[512]{0:T(512)}, f32[512]{0:T(512)S(1)}, u32[]{:S(2)}) copy-start(f32[512]{0:T(512)S(1)} %add_rsqrt_fusion.3) | copy-start | bytes 6148
  35.1 56.0 %copy-start.33 = (f32[512,64]{1,0:T(8,128)}, f32[512,64]{1,0:T(8,128)S(1)}, u32[]{:S(2)}) copy-start(f32[512,64]{1,0:T(8,128)S(1)} %get-tuple-element.68) | copy-start | bytes 393220
  35.1 62.4 %copy-start.22 = (f32[512,64]{1,0:T(8,128)}, f32[512,64]{1,0:T(8,128)S(1)}, u32[]{:S(2)}) copy-start(f32[512,64]{1,0:T(8,128)S(1)} %get-tuple-element.69) | copy-start | bytes 393220
  79.8 4.0 copy-start.3
  80.1 16.8 %copy-start.5 = (f32[64,8,8,128]{3,2,1,0:T(8,128)}, f32[64,8,8,128]{3,2,1,0:T(8,128)S(1)}, u32[]{:S(2)}) copy-start(f32[64,8,8,128]{3,2,1,0:T(8,128)S(1)} %get-tuple-element.45) | copy-start | bytes 6291460
  93.3 5.1 copy-start.35
  93.9 4.5 copy-start.36
  93.9 3.7 copy-start.34
  98.3 8.7 copy-start.26
  98.3 8.7 copy-start.28
  115.3 12.2 copy-start.12
  207.9 47.0 %copy-start.14 = (f32[512,1024]{1,0:T(8,128)S(1)}, f32[512,1024]{1,0:T(8,128)}, u32[]{:S(2)}) copy-start(f32[512,1024]{1,0:T(8,128)} %get-tuple-element.75) | copy-start | bytes 6291460
  272.4 30.1 %copy-start.7 = (f32[512,1024]{1,0:T(8,128)}, f32[512,1024]{1,0:T(8,128)S(1)}, u32[]{:S(2)}) copy-start(f32[512,1024]{1,0:T(8,128)S(1)} %multiply_add_fusion.2) | copy-start | bytes 6291460
  279.0 306.7 %reduce-scatter.15.cloned.1.call-start = ((), (), s32[]{:S(2)}) async-start(), calls=%async_computation.15 | async-start | bytes 12976128 | tf_op jit(solution)/shard_map/reduce_scatter | solution.py:260
  301.6 468.3 %reduce-scatter.9.cloned.1.call-start = ((), (), s32[]{:S(2)}) async-start(), calls=%async_computation.9 | async-start | bytes 17301504 | tf_op jit(solution)/shard_map/reduce_scatter | solution.py:242
  322.5 12.9 copy-start.27
  322.6 12.9 copy-start.29
  335.4 3.4 copy-start.2
  351.0 7.1 copy-start.23
  351.0 7.1 copy-start.32
  373.1 22.2 %copy-start.30 = (bf16[512,1024]{1,0:T(8,128)(2,1)}, bf16[512,1024]{1,0:T(8,128)(2,1)S(1)}, u32[]{:S(2)}) copy-start(bf16[512,1024]{1,0:T(8,128)(2,1)S(1)} %copy.257) | copy-start | bytes 3145732
  373.1 5.3 copy-start.1
  373.1 5.3 copy-start.25
  378.0 5.3 slice-start.2
  378.4 3.7 copy-start.38
  378.4 4.3 copy-start.37
  378.4 4.9 slice-start.3
  385.1 10.1 copy-start.31
  387.4 7.8 copy-start.13
  387.4 7.8 copy-start.40
  387.4 7.8 copy-start.43
  395.2 4.8 copy-start.19
  406.4 614.7 %reduce-scatter.13.cloned.1.call-start = ((), (), s32[]{:S(2)}) async-start(), calls=%async_computation.13 | async-start | bytes 25952256 | tf_op jit(solution)/shard_map/reduce_scatter | solution.py:254
  440.8 12.4 copy-start.48
  440.8 718.5 %reduce-scatter.17.cloned.1.call-start = ((), (), s32[]{:S(2)}) async-start(), calls=%async_computation.17 | async-start | bytes 540672
  453.1 629.4 %copy-start.8 = (f32[512,1024]{1,0:T(8,128)S(1)}, f32[512,1024]{1,0:T(8,128)}, u32[]{:S(2)}) copy-start(f32[512,1024]{1,0:T(8,128)} %copy-done.7) | copy-start | bytes 6291460
  454.3 752.0 %all-gather.22.cloned.1.call-start = ((), (), s32[]{:S(2)}) async-start(), calls=%async_computation.12 | async-start | bytes 2359296 | tf_op jit(solution)/shard_map/all_gather | solution.py:281
  454.9 812.2 %all-gather.26.cloned.1.call-start = ((), (), s32[]{:S(2)}) async-start(), calls=%async_computation.16 | async-start | bytes 3538944 | tf_op jit(solution)/shard_map/all_gather | solution.py:283
  585.7 754.9 %all-gather.20.cloned.1.call-start = ((), (), s32[]{:S(2)}) async-start(), calls=%async_computation.10 | async-start | bytes 4718592 | tf_op jit(solution)/shard_map/all_gather | solution.py:280
  769.9 670.1 %all-gather.24.cloned.1.call-start = ((), (), s32[]{:S(2)}) async-start(), calls=%async_computation.14 | async-start | bytes 7077888 | tf_op jit(solution)/shard_map/all_gather | solution.py:282
  1081.9 374.7 %copy-start.49 = (f32[32,2]{0,1:T(2,128)}, f32[32,2]{0,1:T(2,128)S(1)}, u32[]{:S(2)}) copy-start(f32[32,2]{0,1:T(2,128)S(1)} %reshape.447) | copy-start | bytes 772
  1081.9 4.0 copy-start.16
  1081.9 4.0 copy-start.55
  1176.4 280.8 %copy-start.44 = (f32[256,2]{0,1:T(2,128)}, f32[256,2]{0,1:T(2,128)S(1)}, u32[]{:S(2)}) copy-start(f32[256,2]{0,1:T(2,128)S(1)} %reshape.445) | copy-start | bytes 6148
  1344.4 112.2 %copy-start.52 = (f32[2,2,32]{2,1,0:T(2,128)S(1)}, f32[2,2,32]{2,1,0:T(2,128)}, u32[]{:S(2)}) copy-start(f32[2,2,32]{2,1,0:T(2,128)} %param.31) | copy-start | bytes 1540
  1344.4 112.2 %copy-start.54 = (f32[2,32]{1,0:T(2,128)S(1)}, f32[2,32]{1,0:T(2,128)}, u32[]{:S(2)}) copy-start(f32[2,32]{1,0:T(2,128)} %param.25) | copy-start | bytes 772
  1344.4 112.8 %copy-start.47 = (f32[2,256]{1,0:T(2,128)S(1)}, f32[2,256]{1,0:T(2,128)}, u32[]{:S(2)}) copy-start(f32[2,256]{1,0:T(2,128)} %param.24) | copy-start | bytes 6148
  1344.4 112.8 %copy-start.50 = (f32[2,2,256]{2,1,0:T(2,128)S(1)}, f32[2,2,256]{2,1,0:T(2,128)}, u32[]{:S(2)}) copy-start(f32[2,2,256]{2,1,0:T(2,128)} %param.30) | copy-start | bytes 12292
  1344.4 114.6 %copy-start.10 = (f32[768,1024]{1,0:T(8,128)S(1)}, f32[768,1024]{1,0:T(8,128)}, u32[]{:S(2)}) copy-start(f32[768,1024]{1,0:T(8,128)} %all-gather.26.cloned.1.call-done) | copy-start | bytes 9437188
  1465.1 3.8 slice-start
  1465.1 5.1 slice-start.1
  1501.1 3.7 copy-start.4
  1501.1 5.0 copy-start.9
  (9 other events, 17.6 us)
Sparse Core Ops, SparseCore 0:
  11.3 60.9 all-gather.11
  74.5 34.4 all-gather.13
  111.1 82.0 all-gather.15
  195.2 46.3 all-gather.17
  279.1 149.9 reduce-scatter.10
  434.9 150.6 reduce-scatter.14
  588.0 181.8 reduce-scatter.8
  776.3 244.7 reduce-scatter.12
  1023.9 135.3 reduce-scatter.16
  1161.2 45.0 all-gather.21
  1208.5 58.5 all-gather.25
  1269.1 71.4 all-gather.19
  1342.7 97.2 all-gather.23
where the time goes:
time: 1540 us; the launch traced here: 1530 us
  waiting for transfers between devices  1010 us (66%)
  matrix products  162 us (11%)
  other arithmetic  145 us (9%)
  blocking collectives  94.4 us (6%)
  local copies, waits for them, and re-layouts  91.4 us (6%)
  between operations  20.3 us (1%)
    reduce_scatter x1, waiting for transfers between devices, on_device(): lax.psum_scatter(joined_order(gate_up_local, 0, owners, copies), ('dp', '...  251 us
    reduce_scatter x1, waiting for transfers between devices, on_device(): lax.psum_scatter(joined_order(qkv_local, 0, owners, copies), ('dp', 'grou...  184 us
    reduce_scatter x1, waiting for transfers between devices, on_device(): lax.psum_scatter(joined_order(down_local, 0, owners, copies), ('dp', 'gro...  131 us
    all_gather x1, waiting for transfers between devices, on_device(): lax.all_gather(pieces[2], 'dp', axis=0, tiled=True)  93.9 us
    all_gather x1, waiting for transfers between devices, on_device(): lax.all_gather(pieces[0], 'dp', axis=0, tiled=True)  68.4 us
    unnamed x14, waiting for transfers between devices  66.8 us
    all_gather x1, waiting for transfers between devices, on_device(): lax.all_gather(gate_up_weight.astype(jnp.bfloat16), 'group', axis=0, tile...  59.3 us
    another operation x12, other arithmetic, adam_update(): return (renewed, jnp.stack([first_moment, second]))  57.1 us
  transfers between devices with their start and end apart: 13, of which 11 were waited for; matrix products, arithmetic and copies ran while one was open for 18% of the time, Pallas kernels for 0%

commit v1 on v0

--- a/solution.py
+++ b/solution.py
@@ -104,6 +104,22 @@
     norm_moments,
     head_moments,
 ):
+
+    def place_the_columns(piece_in, mesh_dim, in_dim):
+        n_chips = lax.psum(1, axis_name=mesh_dim)
+        table = [piece_in]
+        for p in tuple(range(1, n_chips)):
+            piece_out = lax.ppermute(
+                table[p - 1],
+                axis_name=mesh_dim,
+                perm=[(i0, (i0 - 1) % n_chips) for i0 in range(n_chips)],
+            )
+            table.append(piece_out)
+        far_arr = jnp.concatenate(table, axis=in_dim)
+        r2 = lax.axis_index(mesh_dim)
+        next_value = jnp.roll(far_arr, r2 * piece_in.shape[in_dim], in_dim)
+        return next_value
+
     full_qkv, full_out, full_gate_up, full_down, full_norm, full_head = (
         lax.all_gather(qkv_weight.astype(jnp.bfloat16), "group", axis=0, tiled=True),
         lax.all_gather(out_weight.astype(jnp.bfloat16), "group", axis=0, tiled=True),
@@ -280,7 +296,7 @@
         lax.all_gather(pieces[0], "dp", axis=0, tiled=True),
         lax.all_gather(pieces[1], "dp", axis=0, tiled=True),
         lax.all_gather(pieces[2], "dp", axis=0, tiled=True),
-        lax.all_gather(pieces[3], "dp", axis=0, tiled=True),
+        place_the_columns(pieces[3], "dp", 0),
         lax.all_gather(pieces[4], "dp", axis=1, tiled=True),
         lax.all_gather(pieces[5], "dp", axis=1, tiled=True),
     )

time: 1540 us -> 1490 us (0.968)
  waiting for transfers between devices: 1010 us -> 929 us
  starting transfers between devices: 0.7 us -> 20.6 us
  local copies, waits for them, and re-layouts: 91.4 us -> 107 us
    all_gather x1 -> x0, waiting for transfers between devices: 56.4 us -> none  [on_device(): lax.all_gather(pieces[3], 'dp', axis=0, tiled=True)]
    unnamed x14 -> x13, waiting for transfers between devices: 66.8 us -> 33.8 us
    reduce_scatter x1, waiting for transfers between devices: 131 us -> 160 us  [on_device(): lax.psum_scatter(joined_order(down_local, 0, owners, copies), ('dp', 'gro...]
    reduce_scatter x1, waiting for transfers between devices: 184 us -> 156 us  [on_device(): lax.psum_scatter(joined_order(qkv_local, 0, owners, copies), ('dp', 'grou...]
    ppermute x0 -> x7, waiting for transfers between devices: none -> 26.5 us  [place_the_columns(): lax.ppermute(table[p - 1], axis_name=mesh_dim, perm=[(i0, (i0 - 1) % n_ch...]
    all_gather x1, waiting for transfers between devices: 29.3 us -> 2.92 us  [on_device(): lax.all_gather(pieces[1], 'dp', axis=0, tiled=True)]
    ppermute x0 -> x7, starting transfers between devices: none -> 20.1 us  [place_the_columns(): lax.ppermute(table[p - 1], axis_name=mesh_dim, perm=[(i0, (i0 - 1) % n_ch...]
    unnamed x135 -> x152, local copies, waits for them, and re-layouts: 33.1 us -> 45.7 us
  transfers between devices with their start and end apart: 13 -> 19, of which waited for: 11 -> 14; matrix products, arithmetic and copies ran while one was open for 18% -> 20% of each run, Pallas kernels for 0% -> 0%
where the time goes in v1:
time: 1490 us; the launch traced here: 1480 us
  waiting for transfers between devices  929 us (62%)
  matrix products  161 us (11%)
  other arithmetic  147 us (10%)
  local copies, waits for them, and re-layouts  107 us (7%)
  blocking collectives  93 us (6%)
  starting transfers between devices  20.6 us (1%)
  between operations  20.4 us (1%)
    reduce_scatter x1, waiting for transfers between devices, on_device(): lax.psum_scatter(joined_order(gate_up_local, 0, owners, copies), ('dp', '...  251 us
    reduce_scatter x1, waiting for transfers between devices, on_device(): lax.psum_scatter(joined_order(down_local, 0, owners, copies), ('dp', 'gro...  160 us
    reduce_scatter x1, waiting for transfers between devices, on_device(): lax.psum_scatter(joined_order(qkv_local, 0, owners, copies), ('dp', 'grou...  156 us
    all_gather x1, waiting for transfers between devices, on_device(): lax.all_gather(pieces[2], 'dp', axis=0, tiled=True)  93.7 us
    all_gather x1, waiting for transfers between devices, on_device(): lax.all_gather(pieces[0], 'dp', axis=0, tiled=True)  73.7 us
    all_gather x1, waiting for transfers between devices, on_device(): lax.all_gather(gate_up_weight.astype(jnp.bfloat16), 'group', axis=0, tile...  58.9 us
    another operation x12, other arithmetic, adam_update(): return (renewed, jnp.stack([first_moment, second]))  57.2 us
    unnamed x152, local copies, waits for them, and re-layouts  45.7 us
  transfers between devices with their start and end apart: 19, of which 14 were waited for; matrix products, arithmetic and copies ran while one was open for 20% of the time, Pallas kernels for 0%

profile of v1, /device:TPU:0, one launch (start us, length us, event | category | flops | bytes accessed | tf_op | source)
XLA Modules:
  0.0 1477.6 jit_solution(9795201867796685306)
XLA Ops:
  7.2 3.9 convert_element_type.111
  12.5 5.0 convert_element_type.126
  19.1 6.0 all_gather.33
  26.8 5.5 all-gather
  35.1 37.2 %all-gather.11.cloned.1.call-done = bf16[1024,4096]{1,0:T(8,128)(2,1)} async-done(((bf16[256,4096]{1,0:T(8,128)(2,1)}), bf16[1024,4096]{1,0:T(8,128)(2,1)}) %all-gather.11.cloned.1.call-update) | async-done | bytes 8388624 | tf_op jit(solution)/shard_map/all_gather | solution.py:124
  72.4 7.4 fusion.62
  80.5 3.2 copy-done.3
  98.5 8.7 fusion.81
  107.2 8.3 exponential_reduce_fusion
  115.6 12.2 fusion.37
  127.8 6.6 multiply_reduce_fusion.9
  134.3 58.9 %all-gather.15.cloned.1.call-done = bf16[1024,6144]{1,0:T(8,128)(2,1)} async-done(((bf16[256,6144]{1,0:T(8,128)(2,1)}), bf16[1024,6144]{1,0:T(8,128)(2,1)}) %all-gather.15.cloned.1.call-update) | async-done | bytes 12582928 | tf_op jit(solution)/shard_map/all_gather | solution.py:126
  193.2 14.6 fusion.79
  207.9 33.8 %all-gather.17.cloned.1.call-done = bf16[3072,1024]{1,0:T(8,128)(2,1)} async-done(((bf16[768,1024]{1,0:T(8,128)(2,1)}), bf16[3072,1024]{1,0:T(8,128)(2,1)}) %all-gather.17.cloned.1.call-update) | async-done | bytes 6291472 | tf_op jit(solution)/shard_map/all_gather | solution.py:127
  241.6 13.0 multiply_convert_fusion.1
  254.7 14.3 multiply_reduce_fusion.6
  269.0 3.2 multiply_add_fusion.2
  274.6 4.2 copy.231
  279.7 5.9 convolution_convert_fusion
  288.6 10.8 fusion
  299.4 12.9 fusion.5
  318.1 4.9 copy.263
  323.0 4.9 copy.264
  327.8 7.3 fusion.36
  336.7 3.2 fusion.54
  340.8 8.7 bitcast_convert_fusion
  350.0 4.7 multiply_subtract_fusion.2
  355.1 3.6 multiply_reduce_fusion.2
  364.7 7.5 fusion.11
  372.3 4.7 fusion.41
  377.0 6.3 copy.230
  384.9 14.9 %fusion.12 = f32[1024,6144]{1,0:T(8,128)} fusion(bf16[512,3072]{1,0:T(8,128)(2,1)} %get-tuple-element.30, bf16[512,3072]{1,0:T(8,128)(2,1)} %get-tuple-element.29, f32[512,1024]{1,0:T(8,128)S(1)} %copy-done.15, f32[1024]{0:T(1024)S(1)} %bitcast.375, f32[512]{0:T(512)S(1)} %add_rsqrt_fusion.2), kind=kOutput, calls=%fused_computation.47 | convolution fusion | flops 6456606720 | bytes 33560576 | tf_op jit(solution)/shard_map/dot_general | solution.py:48
  399.9 17.6 %copy.232 = f32[8,4,32,6144]{3,2,1,0:T(8,128)} copy(f32[8,4,32,6144]{3,2,0,1:T(8,128)} %bitcast.333) | data formatting | bytes 50331648 | tf_op jit(solution)/shard_map/transpose | solution.py:69
  418.7 8.6 fusion.82
  427.2 12.0 copy.233
  440.9 10.9 fusion.29
  453.6 156.4 %reduce-scatter.9.cloned.1.call-done = f32[32,4096]{1,0:T(8,128)} async-done(((f32[1024,4096]{1,0:T(8,128)}), f32[32,4096]{1,0:T(8,128)}) %reduce-scatter.9.cloned.1.call-update) | async-done | bytes 524304 | tf_op jit(solution)/shard_map/reduce_scatter | solution.py:258
  610.1 251.2 %reduce-scatter.13.cloned.1.call-done = f32[32,6144]{1,0:T(8,128)} async-done(((f32[1024,6144]{1,0:T(8,128)}), f32[32,6144]{1,0:T(8,128)}) %reduce-scatter.13.cloned.1.call-update) | async-done | bytes 786448 | tf_op jit(solution)/shard_map/reduce_scatter | solution.py:270
  861.3 160.3 %reduce-scatter.15.cloned.1.call-done = f32[96,1024]{1,0:T(8,128)} async-done(((f32[3072,1024]{1,0:T(8,128)}), f32[96,1024]{1,0:T(8,128)}) %reduce-scatter.15.cloned.1.call-update) | async-done | bytes 393232 | tf_op jit(solution)/shard_map/reduce_scatter | solution.py:276
  1024.5 6.9 collective-permute-done
  1031.4 5.2 collective-permute-start.1
  1036.6 5.7 collective-permute-done.1
  1042.2 5.8 collective-permute-start.2
  1048.1 8.7 add_convert_fusion.1
  1062.4 38.6 %all-reduce = f32[2,128]{1,0:T(2,128)S(1)} all-reduce(f32[2,128]{1,0:T(2,128)S(1)} %reshape.437), channel_id=7, replica_groups=mesh['dp'=8,'group'=4] {'dp','group'}, use_global_device_ids=true, to_apply=%region_22.23.clone | all-reduce | flops 256 | bytes 2048
  1101.1 20.3 %all-gather.2 = f32[8,4,2]{1,2,0:T(2,128)S(1)} all-gather(f32[1,4,2]{1,2,0:T(2,128)S(1)} %dynamic-slice_bitcast_fusion), channel_id=1, replica_groups=mesh['dp'=8,'group'=4] {'dp'}, dimensions={0}, use_global_device_ids=true | all-gather | bytes 288 | tf_op jit(solution)/shard_map/all_gather | solution.py:301
  1124.0 3.1 fusion.28
  1127.1 33.1 %reduce-scatter.17.cloned.1.call-done = f32[32,2]{1,0:T(8,128)} async-done(((f32[1024,2]{1,0:T(8,128)}), f32[32,2]{1,0:T(8,128)}) %reduce-scatter.17.cloned.1.call-update) | async-done | bytes 272
  1161.0 16.3 %all-gather.1 = f32[8,32,2]{1,2,0:T(2,128)S(1)} all-gather(f32[1,32,2]{1,2,0:T(2,128)S(1)} %bitcast.382), channel_id=1, replica_groups=mesh['dp'=8,'group'=4] {'dp'}, dimensions={0}, use_global_device_ids=true | all-gather | bytes 2304 | tf_op jit(solution)/shard_map/all_gather | solution.py:300
  1182.3 4.0 collective-permute-done.5
  1186.3 4.0 collective-permute-start.6
  1193.5 9.9 collective-permute-done.6
  1219.2 73.7 %all-gather.19.cloned.1.call-done = f32[256,4096]{1,0:T(8,128)} async-done(((f32[32,4096]{1,0:T(8,128)}), f32[256,4096]{1,0:T(8,128)}) %all-gather.19.cloned.1.call-update) | async-done | bytes 4194320 | tf_op jit(solution)/shard_map/all_gather | solution.py:296
  1293.0 3.9 multiply_reduce_fusion.1
  1298.5 93.7 %all-gather.23.cloned.1.call-done = f32[256,6144]{1,0:T(8,128)} async-done(((f32[32,6144]{1,0:T(8,128)}), f32[256,6144]{1,0:T(8,128)}) %all-gather.23.cloned.1.call-update) | async-done | bytes 6291472 | tf_op jit(solution)/shard_map/all_gather | solution.py:298
  1392.3 5.0 multiply_reduce_fusion
  1401.7 6.3 psum.7
  1410.0 6.2 fusion.58
  1417.4 3.8 pad_maximum_fusion.3
  1422.6 13.3 fusion.45
  1435.8 10.9 pad_maximum_fusion
  1446.7 6.6 fusion.59
  1458.3 6.9 fusion.53
  1465.2 4.4 pad_maximum_fusion.1
  (255 shorter events, 97.7 us)
Async XLA Ops:
  7.2 4.1 copy-start.17
  7.2 65.2 %all-gather.11.cloned.1.call-start = ((), (), s32[]{:S(2)}) async-start(), calls=%async_computation.5 | async-start | bytes 10485760 | tf_op jit(solution)/shard_map/all_gather | solution.py:124
  11.2 116.6 %all-gather.13.cloned.1.call-start = ((), (), s32[]{:S(2)}) async-start(), calls=%async_computation.6 | async-start | bytes 5242880 | tf_op jit(solution)/shard_map/all_gather | solution.py:125
  12.4 5.2 copy-start.10
  12.4 180.8 %all-gather.15.cloned.1.call-start = ((), (), s32[]{:S(2)}) async-start(), calls=%async_computation.7 | async-start | bytes 15728640 | tf_op jit(solution)/shard_map/all_gather | solution.py:126
  17.5 9.2 copy-start.55
  17.6 14.9 %copy-start.53 = (s32[512]{0:T(512)S(1)}, s32[512]{0:T(512)}, u32[]{:S(2)}) copy-start(s32[512]{0:T(512)} %param.18) | copy-start | bytes 6148
  17.6 14.9 %copy-start.47 = (s32[512]{0:T(512)S(1)}, s32[512]{0:T(512)}, u32[]{:S(2)}) copy-start(s32[512]{0:T(512)} %param.17) | copy-start | bytes 6148
  17.6 224.1 %all-gather.17.cloned.1.call-start = ((), (), s32[]{:S(2)}) async-start(), calls=%async_computation.8 | async-start | bytes 7864320 | tf_op jit(solution)/shard_map/all_gather | solution.py:127
  19.1 434.0 %reduce-scatter.11.cloned.1.call-start = ((), (), s32[]{:S(2)}) async-start(), calls=%async_computation.11 | async-start | bytes 8650752 | tf_op jit(solution)/shard_map/reduce_scatter | solution.py:264
  25.2 54.6 %copy-start.41 = (f32[1,1024]{1,0:T(1,128)}, f32[1,1024]{1,0:T(1,128)S(1)}, u32[]{:S(2)}) copy-start(f32[1,1024]{1,0:T(1,128)S(1)} %get-tuple-element.63) | copy-start | bytes 12292
  26.8 52.9 %copy-start.44 = (f32[512]{0:T(512)}, f32[512]{0:T(512)S(1)}, u32[]{:S(2)}) copy-start(f32[512]{0:T(512)S(1)} %add_rsqrt_fusion.3) | copy-start | bytes 6148
  35.1 56.0 %copy-start.31 = (f32[512,64]{1,0:T(8,128)}, f32[512,64]{1,0:T(8,128)S(1)}, u32[]{:S(2)}) copy-start(f32[512,64]{1,0:T(8,128)S(1)} %get-tuple-element.68) | copy-start | bytes 393220
  79.7 4.0 copy-start.3
  80.0 16.8 %copy-start.5 = (f32[64,8,8,128]{3,2,1,0:T(8,128)}, f32[64,8,8,128]{3,2,1,0:T(8,128)S(1)}, u32[]{:S(2)}) copy-start(f32[64,8,8,128]{3,2,1,0:T(8,128)S(1)} %get-tuple-element.45) | copy-start | bytes 6291460
  93.3 5.0 copy-start.33
  93.8 4.5 copy-start.34
  98.3 8.9 copy-start.24
  98.3 8.9 copy-start.26
  115.6 12.2 copy-start.12
  207.9 46.8 %copy-start.14 = (f32[512,1024]{1,0:T(8,128)S(1)}, f32[512,1024]{1,0:T(8,128)}, u32[]{:S(2)}) copy-start(f32[512,1024]{1,0:T(8,128)} %get-tuple-element.75) | copy-start | bytes 6291460
  272.2 7.5 copy-start.7
  278.8 331.2 %reduce-scatter.9.cloned.1.call-start = ((), (), s32[]{:S(2)}) async-start(), calls=%async_computation.9 | async-start | bytes 17301504 | tf_op jit(solution)/shard_map/reduce_scatter | solution.py:258
  299.4 12.9 copy-start.25
  299.4 12.9 copy-start.27
  327.8 7.3 copy-start.30
  350.0 22.2 %copy-start.28 = (bf16[512,1024]{1,0:T(8,128)(2,1)}, bf16[512,1024]{1,0:T(8,128)(2,1)S(1)}, u32[]{:S(2)}) copy-start(bf16[512,1024]{1,0:T(8,128)(2,1)S(1)} %copy.257) | copy-start | bytes 3145732
  350.0 5.1 copy-start.1
  350.0 5.1 copy-start.23
  354.8 5.3 slice-start.2
  355.1 4.3 copy-start.38
  355.1 4.9 slice-start.3
  362.4 9.8 copy-start.29
  364.7 7.5 copy-start.13
  364.7 7.5 copy-start.42
  364.7 7.5 copy-start.45
  372.2 4.8 copy-start.18
  383.4 477.9 %reduce-scatter.13.cloned.1.call-start = ((), (), s32[]{:S(2)}) async-start(), calls=%async_computation.13 | async-start | bytes 25952256 | tf_op jit(solution)/shard_map/reduce_scatter | solution.py:270
  417.5 604.1 %reduce-scatter.15.cloned.1.call-start = ((), (), s32[]{:S(2)}) async-start(), calls=%async_computation.15 | async-start | bytes 12976128 | tf_op jit(solution)/shard_map/reduce_scatter | solution.py:276
  439.3 12.5 copy-start.50
  439.3 720.9 %reduce-scatter.17.cloned.1.call-start = ((), (), s32[]{:S(2)}) async-start(), calls=%async_computation.16 | async-start | bytes 540672
  453.0 761.8 %all-gather.21.cloned.1.call-start = ((), (), s32[]{:S(2)}) async-start(), calls=%async_computation.12 | async-start | bytes 2359296 | tf_op jit(solution)/shard_map/all_gather | solution.py:297
  453.6 839.4 %all-gather.19.cloned.1.call-start = ((), (), s32[]{:S(2)}) async-start(), calls=%async_computation.10 | async-start | bytes 4718592 | tf_op jit(solution)/shard_map/all_gather | solution.py:296
  610.0 782.2 %all-gather.23.cloned.1.call-start = ((), (), s32[]{:S(2)}) async-start(), calls=%async_computation.14 | async-start | bytes 7077888 | tf_op jit(solution)/shard_map/all_gather | solution.py:298
  1021.6 9.8 collective-permute-start
  1031.4 16.7 %copy-start.36 = (f32[96,1024]{1,0:T(8,128)}, f32[96,1024]{1,0:T(8,128)S(1)}, u32[]{:S(2)}) copy-start(f32[96,1024]{1,0:T(8,128)S(1)} %collective-permute-done) | copy-start | bytes 1179652
  1031.4 10.8 collective-permute-start.1
  1036.6 87.4 %copy-start.8 = (f32[512,1024]{1,0:T(8,128)S(1)}, f32[512,1024]{1,0:T(8,128)}, u32[]{:S(2)}) copy-start(f32[512,1024]{1,0:T(8,128)} %copy-done.7) | copy-start | bytes 6291460
  1042.2 17.8 %collective-permute-start.2 = (f32[96,1024]{1,0:T(8,128)}, f32[96,1024]{1,0:T(8,128)}, u32[]{:S(2)}, u32[]{:S(2)}) collective-permute-start(f32[96,1024]{1,0:T(8,128)} %collective-permute-done.1), channel_id=1, source_target_pairs={{0,28},{4,0},{8,4},{12,8},{16,12},{20,16},{24,20},{28,24},{1,29},{... | collective-permute-start | bytes 1179656 | tf_op jit(solution)/shard_map/ppermute | solution.py:112
  1056.8 123.5 %copy-start.35 = (f32[96,1024]{1,0:T(8,128)S(1)}, f32[96,1024]{1,0:T(8,128)}, u32[]{:S(2)}) copy-start(f32[96,1024]{1,0:T(8,128)} %reduce-scatter.15.cloned.1.call-done) | copy-start | bytes 1179652
  1060.1 62.6 %collective-permute-start.3 = (f32[96,1024]{1,0:T(8,128)}, f32[96,1024]{1,0:T(8,128)}, u32[]{:S(2)}, u32[]{:S(2)}) collective-permute-start(f32[96,1024]{1,0:T(8,128)} %collective-permute-done.2), channel_id=1, source_target_pairs={{0,28},{4,0},{8,4},{12,8},{16,12},{20,16},{24,20},{28,24},{1,29},{... | collective-permute-start | bytes 1179656 | tf_op jit(solution)/shard_map/ppermute | solution.py:112
  1122.7 54.7 %collective-permute-start.4 = (f32[96,1024]{1,0:T(8,128)}, f32[96,1024]{1,0:T(8,128)}, u32[]{:S(2)}, u32[]{:S(2)}) collective-permute-start(f32[96,1024]{1,0:T(8,128)} %collective-permute-done.3), channel_id=1, source_target_pairs={{0,28},{4,0},{8,4},{12,8},{16,12},{20,16},{24,20},{28,24},{1,29},{... | collective-permute-start | bytes 1179656 | tf_op jit(solution)/shard_map/ppermute | solution.py:112
  1127.1 76.3 %copy-start.37 = (f32[96,1024]{1,0:T(8,128)S(1)}, f32[96,1024]{1,0:T(8,128)}, u32[]{:S(2)}) copy-start(f32[96,1024]{1,0:T(8,128)} %copy-done.36) | copy-start | bytes 1179652
  1177.4 232.0 %copy-start.46 = (f32[256,2]{0,1:T(2,128)}, f32[256,2]{0,1:T(2,128)S(1)}, u32[]{:S(2)}) copy-start(f32[256,2]{0,1:T(2,128)S(1)} %reshape.445) | copy-start | bytes 6148
  1177.4 8.9 collective-permute-start.5
  1186.3 17.0 %collective-permute-start.6 = (f32[96,1024]{1,0:T(8,128)S(1)}, f32[96,1024]{1,0:T(8,128)S(1)}, u32[]{:S(2)}, u32[]{:S(2)}) collective-permute-start(f32[96,1024]{1,0:T(8,128)S(1)} %collective-permute-done.5), channel_id=1, source_target_pairs={{0,28},{4,0},{8,4},{12,8},{16,12},{20,16},{24,20},{28,24},{1,29},{... | collective-permute-start | bytes 1179656 | tf_op jit(solution)/shard_map/ppermute | solution.py:112
  1296.8 112.0 %copy-start.51 = (f32[32,2]{0,1:T(2,128)S(1)}, f32[32,2]{0,1:T(2,128)}, u32[]{:S(2)}) copy-start(f32[32,2]{0,1:T(2,128)} %reshape.447) | copy-start | bytes 772
  1296.8 112.0 %copy-start.54 = (f32[2,2,32]{2,1,0:T(2,128)S(1)}, f32[2,2,32]{2,1,0:T(2,128)}, u32[]{:S(2)}) copy-start(f32[2,2,32]{2,1,0:T(2,128)} %param.31) | copy-start | bytes 1540
  1296.8 112.0 %copy-start.56 = (f32[2,32]{1,0:T(2,128)S(1)}, f32[2,32]{1,0:T(2,128)}, u32[]{:S(2)}) copy-start(f32[2,32]{1,0:T(2,128)} %param.25) | copy-start | bytes 772
  1296.8 112.6 %copy-start.49 = (f32[2,256]{1,0:T(2,128)S(1)}, f32[2,256]{1,0:T(2,128)}, u32[]{:S(2)}) copy-start(f32[2,256]{1,0:T(2,128)} %param.24) | copy-start | bytes 6148
  1296.8 112.6 %copy-start.52 = (f32[2,2,256]{2,1,0:T(2,128)S(1)}, f32[2,2,256]{2,1,0:T(2,128)}, u32[]{:S(2)}) copy-start(f32[2,2,256]{2,1,0:T(2,128)} %param.30) | copy-start | bytes 12292
  1296.8 113.2 %copy-start.11 = (f32[768,1024]{1,0:T(8,128)S(1)}, f32[768,1024]{1,0:T(8,128)}, u32[]{:S(2)}) copy-start(f32[768,1024]{1,0:T(8,128)} %param.23) | copy-start | bytes 9437188
  1417.4 5.1 slice-start.1
  1453.3 5.0 copy-start.9
  (16 other events, 39.9 us)
Sparse Core Ops, SparseCore 0:
  11.3 60.9 all-gather.10
  74.5 34.4 all-gather.12
  111.1 82.0 all-gather.14
  195.2 46.3 all-gather.16
  278.9 150.1 reduce-scatter.10
  431.2 178.7 reduce-scatter.8
  616.4 244.7 reduce-scatter.12
  867.3 154.2 reduce-scatter.14
  1024.4 135.7 reduce-scatter.16
  1162.2 52.5 all-gather.20
  1216.9 75.9 all-gather.18
  1295.0 97.2 all-gather.22
